TPU v7x, 32 devices: a whole 2x2x4 slice. The times are simulated.
32 devices in a mesh: mem: 8 (over y, x, core), pix: 4 (over z).
Axes of the slice: x: 2, y: 2, z: 4, core: 2. Of those that a mesh axis runs over, the one named last changes fastest.
Arguments:
- prior_motion: bfloat16 [64, 16, 131072], P('mem', None, 'pix'), may hold values from -6 to 6
- measured_motion: float32 [1200], replicated, may hold values from -1.6 to 1.6
- measurement_noise_stddev: float32 [1200], replicated, may hold values from 0.05 to 0.5
- gaussian_jitter: float32 [2, 1200, 64], replicated, may hold values from -6 to 6
- scene_couples: int32 [2, 1200], replicated, may hold values from 0 to 15, as said below
- targeted_tile_number: int32 [1200], replicated, may hold values from 0 to 2047
Outputs:
- analysis: bfloat16 [64, 16, 131072], P('mem', None, 'pix')
Inputs may be any that keep to these rules, and one draw needn't show every extreme that they name: scene_couples[0, k] < scene_couples[1, k]: row 0 holds the earlier acquisition, row 1 the later.
All inputs are finite; a program needn't handle non-finite values.
Results may differ from a plain program's by a relative error of at most 0.011.
Values may be sent and summed in bfloat16 or wider, within the bound.
A program may use at most 192 MiB of HBM per device.

v0:
```python
import math
import jax
import jax.numpy as jnp
from jax import lax
from jax.sharding import PartitionSpec as P

BLK = 64
PASS_COUNT = 2


def block_sums(pieces):
    part_cells = pieces.shape[2]
    block_count = part_cells // BLK
    summer = (
        jnp.arange(part_cells, dtype=jnp.int32)[:, None] // BLK
        == jnp.arange(block_count, dtype=jnp.int32)[None, :]
    ).astype(jnp.bfloat16)
    flat = jnp.dot(pieces.reshape(-1, part_cells), summer, preferred_element_type=jnp.float32)
    return flat.reshape(pieces.shape[0], pieces.shape[1], block_count)


def with_sums(pieces):
    return (pieces, block_sums(pieces))


def to_pixels(ground_motion_vector):
    return with_sums(
        lax.all_to_all(ground_motion_vector, "mem", split_axis=2, concat_axis=0, tiled=True)
    )


def to_members(pixel_state):
    return lax.all_to_all(pixel_state, "mem", split_axis=0, concat_axis=2, tiled=True)


def predict(sums, picker):
    flat_sums = sums.reshape(sums.shape[0], -1)
    return (
        jnp.dot(
            picker, flat_sums.T, precision=lax.Precision.HIGHEST, preferred_element_type=jnp.float32
        )
        / BLK
    )


def member_terms(predicted, measured_motion, member_anomaly, noise):
    realization_vectors = predicted.shape[1]
    centred = predicted - jnp.mean(predicted, axis=1, keepdims=True)
    scaled = centred / (member_anomaly[:, None] * math.sqrt(realization_vectors - 1))
    misfit = (
        measured_motion[:, None] + member_anomaly[:, None] * noise - predicted
    ) / member_anomaly[:, None]
    return (scaled, misfit)


def products(scaled, misfit):
    gram = jnp.dot(
        scaled.T, scaled, precision=lax.Precision.HIGHEST, preferred_element_type=jnp.float32
    )
    cross = jnp.dot(
        scaled.T, misfit, precision=lax.Precision.HIGHEST, preferred_element_type=jnp.float32
    )
    return (gram, cross)


def solve_mixing(gram, cross):
    realization_vectors = gram.shape[0]
    factor = jnp.linalg.cholesky(jnp.eye(realization_vectors, dtype=jnp.float32) + gram)
    return (
        jax.scipy.linalg.cho_solve((factor, True), cross) / math.sqrt(realization_vectors - 1)
    ).astype(jnp.bfloat16)


def update(pixel_state, mixing):
    realization_vectors = pixel_state.shape[0]
    average = jnp.sum(pixel_state, axis=0, dtype=jnp.float32) / realization_vectors
    anomaly = (pixel_state.astype(jnp.float32) - average).astype(jnp.bfloat16)
    change = jnp.dot(
        mixing.T, anomaly.reshape(realization_vectors, -1), preferred_element_type=jnp.float32
    )
    return (pixel_state.astype(jnp.float32) + change.reshape(pixel_state.shape)).astype(
        jnp.bfloat16
    )


def body(
    prior_motion,
    measured_motion,
    measurement_noise_stddev,
    gaussian_jitter,
    scene_couples,
    targeted_tile_number,
):
    cells_per_tile = prior_motion.shape[2]
    part_width = cells_per_tile // lax.axis_size("mem")
    local_blocks = part_width // BLK
    first_block = (
        lax.axis_index("pix") * cells_per_tile + lax.axis_index("mem") * part_width
    ) // BLK
    block_range = first_block + jnp.arange(local_blocks, dtype=jnp.int32)
    block_table = (targeted_tile_number[:, None] == block_range[None, :]).astype(jnp.float32)
    scene_timeline = jnp.arange(prior_motion.shape[1], dtype=jnp.int32)
    pair_table = (scene_timeline[None, :] == scene_couples[1][:, None]).astype(jnp.float32) - (
        scene_timeline[None, :] == scene_couples[0][:, None]
    ).astype(jnp.float32)
    picker = (pair_table[:, :, None] * block_table[:, None, :]).reshape(pair_table.shape[0], -1)
    member_anomaly = jnp.sqrt(jnp.float32(float(PASS_COUNT))) * measurement_noise_stddev
    pixel_state, sums = to_pixels(prior_motion)
    for iteration in range(PASS_COUNT):
        if iteration > 0:
            sums = block_sums(pixel_state)
        predicted = predict(sums, picker)
        predicted = lax.psum(predicted, ("mem", "pix"))
        scaled, misfit = member_terms(
            predicted, measured_motion, member_anomaly, gaussian_jitter[iteration]
        )
        gram, cross = products(scaled, misfit)
        pixel_state = update(pixel_state, solve_mixing(gram, cross))
    return to_members(pixel_state)


def solution(mesh):
    return jax.shard_map(
        body,
        mesh=mesh,
        in_specs=(P("mem", None, "pix"), P(), P(), P(), P(), P()),
        out_specs=P("mem", None, "pix"),
        check_vma=False,
    )
```

profile of v0, /device:TPU:8, one launch (start us, length us, event | category | flops | bytes accessed | tf_op | source)
XLA Modules:
  0.0 957.3 jit_solution(7385386645052010220)
XLA Ops:
  6.5 52.6 %copy.41 = bf16[8,16,32768]{1,0,2:T(8,128)(2,1)} copy(bf16[8,16,32768]{2,1,0:T(8,128)(2,1)} %param.9) | data formatting | bytes 16777216 | tf_op args[0]
  59.1 103.9 %reshape.195 = bf16[8,2,262144]{2,1,0:T(2,128)(2,1)} reshape(bf16[32768,8,16]{2,1,0:T(8,128)(2,1)} %bitcast.86) | data formatting | bytes 16777216
  163.1 0.0 copy-start
  163.1 0.0 copy-start.1
  163.1 0.0 copy-start.2
  163.1 5.1 all-to-all-start
  168.2 0.5 all-reduce.3.cloned.1.call-start
  168.7 0.0 copy-done
  168.8 0.0 copy-done.1
  168.8 0.0 copy-done.2
  168.8 0.1 compare_convert_fusion
  168.9 2.9 broadcast_multiply_fusion
  171.8 90.4 %all-to-all-done = bf16[8,2,262144]{2,1,0:T(2,128)(2,1)} async-done(((bf16[8,2,262144]{2,1,0:T(2,128)(2,1)}), bf16[8,2,262144]{2,1,0:T(2,128)(2,1)}, u32[]{:S(2)}, u32[]{:S(2)}) %all-to-all-start) | async-done | bytes 8388640 | tf_op jit(solution)/shard_map/all_to_all | solution.py:28
  262.2 80.3 %reshape.196 = bf16[32768,8,16]{2,1,0:T(8,128)(2,1)} reshape(bf16[8,2,262144]{2,1,0:T(2,128)(2,1)} %all-to-all-done) | data formatting | bytes 16777216
  342.5 52.2 %copy.65 = bf16[8,16,8,4096]{3,2,1,0:T(8,128)(2,1)} copy(bf16[8,16,8,4096]{1,0,3,2:T(8,128)(2,1)} %bitcast) | data formatting | bytes 16777216 | tf_op jit(solution)/shard_map/all_to_all | solution.py:28
  394.7 11.4 %bitcast_convert_fusion = f32[8,8,16,4096]{3,0,2,1:T(8,128)} fusion(bf16[8,16,8,4096]{3,2,1,0:T(8,128)(2,1)} %copy.65), kind=kLoop, calls=%fused_computation.14 | loop fusion | flops 4194304 | bytes 25165824 | tf_op jit(solution)/shard_map/convert_element_type | solution.py:81
  406.1 5.2 fusion.8
  411.3 60.0 %copy.44 = bf16[8,8,16,4096]{3,2,1,0:T(8,128)(2,1)} copy(bf16[8,8,16,4096]{2,1,3,0:T(8,128)(2,1)} %bitcast.4) | data formatting | bytes 16777216 | tf_op jit(solution)/shard_map/all_to_all | solution.py:28
  471.3 6.5 convolution_bitcast_fusion
  477.8 0.2 copy.45
  478.0 0.2 reshape_reshape.6
  478.2 6.6 convolution_multiply_fusion.1
  484.8 0.0 all-reduce.3.cloned.1.call-update
  484.9 0.0 all-reduce.5.cloned.1.call-start
  484.9 15.2 %copy.90 = f32[8,8,16,4096]{3,2,1,0:T(8,128)S(1)} copy(f32[8,8,16,4096]{3,0,2,1:T(8,128)} %bitcast_convert_fusion) | data formatting | bytes 33554432 | tf_op jit(solution)/shard_map/convert_element_type | solution.py:81
  500.1 10.9 %copy.73 = f32[8,8,16,4096]{3,1,2,0:T(8,128)S(1)} copy(f32[8,8,16,4096]{3,2,1,0:T(8,128)S(1)} %copy.90) | data formatting | bytes 33554432
  511.1 0.1 copy.74
  511.1 0.0 copy-start.3
  511.1 0.0 copy-start.4
  511.2 3.9 subtract_convert_fusion
  515.0 98.2 %all-reduce.3.cloned.1.call-done = f32[1200,64]{0,1:T(8,128)} async-done(((f32[1200,64]{0,1:T(8,128)}), f32[1200,64]{0,1:T(8,128)}) %all-reduce.3.cloned.1.call-update) | async-done | bytes 307216 | tf_op jit(solution)/shard_map/psum | solution.py:113
  613.2 1.0 reduce_sum.36
  614.3 1.5 convolution_add_fusion.1
  615.8 0.1 copy.47
  615.9 5.8 cholesky.44
  621.8 0.7 compare_reduce_fusion.1
  622.5 0.7 fusion.42
  623.2 4.9 custom-call.8
  628.1 0.0 copy-done.3
  628.1 0.0 copy-done.4
  628.1 1.5 fusion.26
  629.7 0.2 fusion.49
  629.9 0.2 fusion.14
  630.1 21.8 %convert_reduce_fusion = (f32[16,4096]{1,0:T(8,128)S(1)}, bf16[64,16,4096]{2,0,1:T(8,128)(2,1)}) fusion(bf16[64,64,1]{1,0,2:T(8,128)(2,1)S(1)} %fusion.14, bf16[8,16,8,4096]{3,2,1,0:T(8,128)(2,1)} %bitcast.113, f32[8,8,16,4096]{3,0,2,1:T(8,128)} %bitcast_convert_fusion), kind=kOutput, calls=%fused_computation.2 | convolution fusion | flops 553582592 | bytes 33824768 | tf_op jit(solution)/shard_map/dot_general | solution.py:78
  651.9 11.4 %copy.51 = bf16[64,16,4096]{2,1,0:T(8,128)(2,1)} copy(bf16[64,16,4096]{2,0,1:T(8,128)(2,1)} %get-tuple-element.12) | data formatting | bytes 16777216 | tf_op jit(solution)/shard_map/convert_element_type | solution.py:81
  663.2 5.8 fusion.9
  669.0 0.2 reshape_reshape.7
  669.2 6.6 convolution_multiply_fusion
  675.9 0.0 all-reduce.5.cloned.1.call-update
  675.9 128.1 %all-reduce.5.cloned.1.call-done = f32[1200,64]{0,1:T(8,128)} async-done(((f32[1200,64]{0,1:T(8,128)}), f32[1200,64]{0,1:T(8,128)}) %all-reduce.5.cloned.1.call-update) | async-done | bytes 307216 | tf_op jit(solution)/shard_map/psum | solution.py:113
  804.0 1.0 reduce_sum.38
  805.0 1.5 convolution_add_fusion
  806.5 0.1 copy.54
  806.6 5.8 cholesky.55
  812.5 0.6 compare_reduce_fusion
  813.2 0.7 fusion.43
  813.8 5.0 custom-call.9
  818.8 1.5 fusion.21
  820.4 0.2 fusion.45
  820.6 0.2 fusion.13
  820.8 10.6 %fusion.1 = bf16[64,16,4096]{2,0,1:T(8,128)(2,1)} fusion(bf16[64,16,4096]{2,0,1:T(8,128)(2,1)} %get-tuple-element.12, bf16[64,64,1]{1,0,2:T(8,128)(2,1)S(1)} %fusion.13, f32[16,4096]{1,0:T(8,128)S(1)} %broadcast_multiply_fusion.1), kind=kOutput, calls=%fused_computation.4 | convolution fusion | flops 562036736 | bytes 17047552 | tf_op jit(solution)/shard_map/dot_general | solution.py:78
  831.4 11.2 %copy.58 = bf16[64,16,4096]{2,1,0:T(8,128)(2,1)} copy(bf16[64,16,4096]{2,0,1:T(8,128)(2,1)} %fusion.1) | data formatting | bytes 16777216 | tf_op jit(solution)/shard_map/convert_element_type | solution.py:81
  842.6 99.7 %all_to_all.33 = bf16[64,16,4096]{2,1,0:T(8,128)(2,1)} all-to-all(bf16[64,16,4096]{2,1,0:T(8,128)(2,1)} %copy.58), channel_id=1, replica_groups=mesh['mem'=8,'pix'=4] {'mem'}, dimensions={0} | all-to-all | bytes 16777216 | tf_op jit(solution)/shard_map/all_to_all | solution.py:33
  942.3 7.9 copy.72
  (13 shorter events, 0.2 us)
Async XLA Ops:
  163.1 5.7 copy-start
  163.1 5.7 copy-start.1
  163.1 5.7 copy-start.2
  163.1 99.1 %all-to-all-start = ((bf16[8,2,262144]{2,1,0:T(2,128)(2,1)}), bf16[8,2,262144]{2,1,0:T(2,128)(2,1)}, u32[]{:S(2)}, u32[]{:S(2)}) async-start(bf16[8,2,262144]{2,1,0:T(2,128)(2,1)} %reshape.195), calls=%async_computation | async-start | bytes 16777216 | tf_op jit(solution)/shard_map/all_to_all | solution.py:28
  168.2 445.1 %all-reduce.3.cloned.1.call-start = ((), (), s32[]{:S(2)}) async-start(), calls=%async_computation.2 | async-start | bytes 655360 | tf_op jit(solution)/shard_map/psum | solution.py:113
  484.9 319.1 %all-reduce.5.cloned.1.call-start = ((), (), s32[]{:S(2)}) async-start(), calls=%async_computation.3 | async-start | bytes 655360 | tf_op jit(solution)/shard_map/psum | solution.py:113
  511.1 117.0 %copy-start.3 = (f32[2,1200,64]{1,2,0:T(8,128)S(1)}, f32[2,1200,64]{1,2,0:T(8,128)}, u32[]{:S(2)}) copy-start(f32[2,1200,64]{1,2,0:T(8,128)} %param.12) | copy-start | bytes 1843204
  511.1 117.0 %copy-start.4 = (f32[1200]{0:T(1024)S(1)}, f32[1200]{0:T(1024)}, u32[]{:S(2)}) copy-start(f32[1200]{0:T(1024)} %param.10) | copy-start | bytes 14404
Sparse Core Ops, SparseCore 0:
  485.0 128.2 all-reduce.2
  676.0 127.9 all-reduce.4
where the time goes:
time: 970 us; the launch traced here: 957 us
  local copies, waits for them, and re-layouts  406 us (42%)
  waiting for transfers between devices  317 us (33%)
  blocking collectives  99.7 us (10%)
  matrix products  64.9 us (7%)
  other arithmetic  49.9 us (5%)
  between operations  13.9 us (1%)
    unnamed x15, local copies, waits for them, and re-layouts  248 us
    psum x2, waiting for transfers between devices, body(): predicted = lax.psum(predicted, ('mem', 'pix'))  226 us
    all_to_all x2, local copies, waits for them, and re-layouts, to_pixels(): lax.all_to_all(ground_motion_vector, 'mem', split_axis=2, concat_axis=0,...  112 us
    all_to_all x1, blocking collectives, to_members(): lax.all_to_all(pixel_state, 'mem', split_axis=0, concat_axis=2, tiled=True)  99.7 us
    all_to_all x1, waiting for transfers between devices, to_pixels(): lax.all_to_all(ground_motion_vector, 'mem', split_axis=2, concat_axis=0,...  90.4 us
    dot_general x2, matrix products, update(): jnp.dot(mixing.T, anomaly.reshape(realization_vectors, -1), preferred_ele...  32.4 us
    convert_element_type x2, local copies, waits for them, and re-layouts, update(): (pixel_state.astype(jnp.float32) + change.reshape(pixel_state.shape)).ast...  22.6 us
  transfers between devices with their start and end apart: 3, of which 3 were waited for; matrix products, arithmetic and copies ran while one was open for 3% of the time, Pallas kernels for 0%

commit v1 on v0

--- a/solution.py
+++ b/solution.py
@@ -110,7 +110,7 @@
         if iteration > 0:
             sums = block_sums(pixel_state)
         predicted = predict(sums, picker)
-        predicted = lax.psum(predicted, ("mem", "pix"))
+        predicted = jnp.sum(lax.all_gather(predicted, ("mem", "pix")), axis=0)
         scaled, misfit = member_terms(
             predicted, measured_motion, member_anomaly, gaussian_jitter[iteration]
         )

time: 970 us -> 838 us (0.86)
  waiting for transfers between devices: 317 us -> 176 us
  other arithmetic: 49.9 us -> 59.6 us
    psum x2 -> x0, waiting for transfers between devices: 226 us -> none  [body(): predicted = lax.psum(predicted, ('mem', 'pix'))]
    all_gather x0 -> x2, waiting for transfers between devices: none -> 85.8 us  [body(): predicted = jnp.sum(lax.all_gather(predicted, ('mem', 'pix')), axis=0)]
    unnamed x15 -> x19, local copies, waits for them, and re-layouts: 248 us -> 249 us
  transfers between devices with their start and end apart: 3 -> 3, of which waited for: 3 -> 2; matrix products, arithmetic and copies ran while one was open for 3% -> 13% of each run, Pallas kernels for 0% -> 0%
where the time goes in v1:
time: 838 us; the launch traced here: 824 us
  local copies, waits for them, and re-layouts  408 us (49%)
  waiting for transfers between devices  176 us (21%)
  blocking collectives  99.7 us (12%)
  matrix products  60.2 us (7%)
  other arithmetic  59.6 us (7%)
  between operations  14.2 us (2%)
    unnamed x19, local copies, waits for them, and re-layouts  249 us
    all_to_all x2, local copies, waits for them, and re-layouts, to_pixels(): lax.all_to_all(ground_motion_vector, 'mem', split_axis=2, concat_axis=0,...  112 us
    all_to_all x1, blocking collectives, to_members(): lax.all_to_all(pixel_state, 'mem', split_axis=0, concat_axis=2, tiled=True)  99.7 us
    all_to_all x1, waiting for transfers between devices, to_pixels(): lax.all_to_all(ground_motion_vector, 'mem', split_axis=2, concat_axis=0,...  90.6 us
    all_gather x2, waiting for transfers between devices, body(): predicted = jnp.sum(lax.all_gather(predicted, ('mem', 'pix')), axis=0)  85.8 us
    dot_general x2, matrix products, update(): jnp.dot(mixing.T, anomaly.reshape(realization_vectors, -1), preferred_ele...  32.2 us
    convert_element_type x2, local copies, waits for them, and re-layouts, update(): (pixel_state.astype(jnp.float32) + change.reshape(pixel_state.shape)).ast...  22.6 us
  transfers between devices with their start and end apart: 3, of which 2 were waited for; matrix products, arithmetic and copies ran while one was open for 13% of the time, Pallas kernels for 0%

profile of v1, /device:TPU:8, one launch (start us, length us, event | category | flops | bytes accessed | tf_op | source)
XLA Modules:
  0.0 823.6 jit_solution(8260455380296624256)
XLA Ops:
  6.5 52.6 %copy.41 = bf16[8,16,32768]{1,0,2:T(8,128)(2,1)} copy(bf16[8,16,32768]{2,1,0:T(8,128)(2,1)} %param.9) | data formatting | bytes 16777216 | tf_op args[0]
  59.1 103.9 %reshape.209 = bf16[8,2,262144]{2,1,0:T(2,128)(2,1)} reshape(bf16[32768,8,16]{2,1,0:T(8,128)(2,1)} %bitcast.90) | data formatting | bytes 16777216
  163.1 5.1 all-to-all-start
  168.2 0.3 all-gather.7.cloned.1.call-start
  168.5 0.0 copy-done
  168.5 0.0 copy-done.2
  168.6 0.1 compare_convert_fusion
  168.6 3.0 broadcast_multiply_fusion
  171.6 90.6 %all-to-all-done = bf16[8,2,262144]{2,1,0:T(2,128)(2,1)} async-done(((bf16[8,2,262144]{2,1,0:T(2,128)(2,1)}), bf16[8,2,262144]{2,1,0:T(2,128)(2,1)}, u32[]{:S(2)}, u32[]{:S(2)}) %all-to-all-start) | async-done | bytes 8388640 | tf_op jit(solution)/shard_map/all_to_all | solution.py:28
  262.2 80.3 %reshape.210 = bf16[32768,8,16]{2,1,0:T(8,128)(2,1)} reshape(bf16[8,2,262144]{2,1,0:T(2,128)(2,1)} %all-to-all-done) | data formatting | bytes 16777216
  342.5 60.0 %copy.44 = bf16[8,8,16,4096]{3,2,1,0:T(8,128)(2,1)} copy(bf16[8,8,16,4096]{2,1,3,0:T(8,128)(2,1)} %bitcast.4) | data formatting | bytes 16777216 | tf_op jit(solution)/shard_map/all_to_all | solution.py:28
  402.5 6.3 convolution_bitcast_fusion
  408.8 0.2 copy.45
  409.0 0.2 reshape_reshape.6
  409.2 6.6 fusion.9
  415.8 0.0 all-gather.7.cloned.1.call-update
  415.9 0.4 all-gather.9.cloned.1.call-start
  416.3 0.0 copy-done.1
  416.3 52.4 %copy.65 = bf16[8,16,8,4096]{3,2,1,0:T(8,128)(2,1)} copy(bf16[8,16,8,4096]{1,0,3,2:T(8,128)(2,1)} %bitcast) | data formatting | bytes 16777216 | tf_op jit(solution)/shard_map/all_to_all | solution.py:28
  468.8 11.4 %bitcast_convert_fusion = f32[8,8,16,4096]{3,0,2,1:T(8,128)} fusion(bf16[8,16,8,4096]{3,2,1,0:T(8,128)(2,1)} %copy.65), kind=kLoop, calls=%fused_computation.14 | loop fusion | flops 4194304 | bytes 25165824 | tf_op jit(solution)/shard_map/convert_element_type | solution.py:81
  480.2 15.3 %copy.90 = f32[8,8,16,4096]{3,2,1,0:T(8,128)S(1)} copy(f32[8,8,16,4096]{3,0,2,1:T(8,128)} %bitcast_convert_fusion) | data formatting | bytes 33554432 | tf_op jit(solution)/shard_map/convert_element_type | solution.py:81
  495.6 0.0 slice-start.1
  495.6 11.7 %copy.73 = f32[8,8,16,4096]{3,1,2,0:T(8,128)} copy(f32[8,8,16,4096]{3,2,1,0:T(8,128)S(1)} %copy.90) | data formatting | bytes 33554432
  507.3 0.0 slice-done
  507.3 0.0 slice-done.1
  507.3 1.8 fusion.8
  509.2 0.1 copy.74
  509.3 9.1 %subtract_convert_fusion = bf16[64,65536]{1,0:T(8,128)(2,1)} fusion(f32[64,65536]{1,0:T(8,128)} %bitcast.115, f32[65536]{0:T(1024)S(1)} %bitcast.122), kind=kLoop, calls=%fused_computation.8 | loop fusion | flops 8388608 | bytes 25427968 | tf_op jit(solution)/shard_map/convert_element_type | solution.py:77
  518.4 0.0 copy-start.3
  518.4 0.0 copy-start.4
  518.4 0.0 all-gather.7.cloned.1.call-done
  518.4 4.9 fusion.58
  523.4 0.4 convolution_add_fusion.1
  523.8 0.1 copy.47
  523.9 5.8 cholesky.44
  529.8 0.6 compare_reduce_fusion.1
  530.4 0.6 fusion.44
  531.0 4.9 custom-call.8
  535.9 0.0 copy-done.3
  535.9 0.0 copy-done.4
  535.9 0.5 fusion.28
  536.4 0.2 fusion.51
  536.6 0.2 fusion.16
  536.8 21.6 %convert_reduce_fusion = (f32[16,4096]{1,0:T(8,128)S(1)}, bf16[64,16,4096]{2,0,1:T(8,128)(2,1)}) fusion(bf16[64,64,1]{1,0,2:T(8,128)(2,1)S(1)} %fusion.16, bf16[8,16,8,4096]{3,2,1,0:T(8,128)(2,1)} %bitcast.119, f32[8,8,16,4096]{3,0,2,1:T(8,128)} %bitcast_convert_fusion), kind=kOutput, calls=%fused_computation.2 | convolution fusion | flops 553582592 | bytes 33824768 | tf_op jit(solution)/shard_map/dot_general | solution.py:78
  558.4 11.4 %copy.51 = bf16[64,16,4096]{2,1,0:T(8,128)(2,1)} copy(bf16[64,16,4096]{2,0,1:T(8,128)(2,1)} %get-tuple-element.16) | data formatting | bytes 16777216 | tf_op jit(solution)/shard_map/convert_element_type | solution.py:81
  569.7 5.8 fusion.11
  575.6 0.2 reshape_reshape.7
  575.7 6.6 fusion.10
  582.4 0.0 all-gather.9.cloned.1.call-update
  582.4 85.8 %all-gather.9.cloned.1.call-done = f32[32,1200,64]{1,2,0:T(8,128)} async-done(((f32[1,1200,64]{1,2,0:T(8,128)}), f32[32,1200,64]{1,2,0:T(8,128)}) %all-gather.9.cloned.1.call-update) | async-done | bytes 9830416 | tf_op jit(solution)/shard_map/all_gather | solution.py:113
  668.2 4.9 fusion.57
  673.1 0.4 convolution_add_fusion
  673.5 0.5 fusion.23
  674.0 0.1 copy.54
  674.1 6.1 cholesky.55
  680.2 0.6 compare_reduce_fusion
  680.9 0.7 fusion.45
  681.5 4.9 custom-call.9
  686.4 0.3 fusion.47
  686.7 0.2 fusion.15
  686.9 10.6 %fusion.1 = bf16[64,16,4096]{2,0,1:T(8,128)(2,1)} fusion(bf16[64,16,4096]{2,0,1:T(8,128)(2,1)} %get-tuple-element.16, bf16[64,64,1]{1,0,2:T(8,128)(2,1)S(1)} %fusion.15, f32[16,4096]{1,0:T(8,128)S(1)} %broadcast_multiply_fusion.1), kind=kOutput, calls=%fused_computation.4 | convolution fusion | flops 562036736 | bytes 17047552 | tf_op jit(solution)/shard_map/dot_general | solution.py:78
  697.5 11.2 %copy.58 = bf16[64,16,4096]{2,1,0:T(8,128)(2,1)} copy(bf16[64,16,4096]{2,0,1:T(8,128)(2,1)} %fusion.1) | data formatting | bytes 16777216 | tf_op jit(solution)/shard_map/convert_element_type | solution.py:81
  708.7 99.7 %all_to_all.33 = bf16[64,16,4096]{2,1,0:T(8,128)(2,1)} all-to-all(bf16[64,16,4096]{2,1,0:T(8,128)(2,1)} %copy.58), channel_id=1, replica_groups=mesh['mem'=8,'pix'=4] {'mem'}, dimensions={0} | all-to-all | bytes 16777216 | tf_op jit(solution)/shard_map/all_to_all | solution.py:33
  808.4 7.9 copy.72
  (18 shorter events, 0.2 us)
Async XLA Ops:
  163.1 5.4 copy-start
  163.1 5.5 copy-start.2
  163.1 99.1 %all-to-all-start = ((bf16[8,2,262144]{2,1,0:T(2,128)(2,1)}), bf16[8,2,262144]{2,1,0:T(2,128)(2,1)}, u32[]{:S(2)}, u32[]{:S(2)}) async-start(bf16[8,2,262144]{2,1,0:T(2,128)(2,1)} %reshape.209), calls=%async_computation | async-start | bytes 16777216 | tf_op jit(solution)/shard_map/all_to_all | solution.py:28
  168.2 350.2 %all-gather.7.cloned.1.call-start = ((), (), s32[]{:S(2)}) async-start(), calls=%async_computation.2 | async-start | bytes 10813440 | tf_op jit(solution)/shard_map/all_gather | solution.py:113
  402.5 13.8 %copy-start.1 = (f32[1200]{0:T(1024)S(1)}, f32[1200]{0:T(1024)}, u32[]{:S(2)}) copy-start(f32[1200]{0:T(1024)} %param.11) | copy-start | bytes 14404
  415.9 252.3 %all-gather.9.cloned.1.call-start = ((), (), s32[]{:S(2)}) async-start(), calls=%async_computation.3 | async-start | bytes 10813440 | tf_op jit(solution)/shard_map/all_gather | solution.py:113
  480.2 27.1 %slice-start = ((s8[8388608]{0:T(1024)(128)(4,1)}), s8[4194304]{0:T(1024)(128)(4,1)S(1)}, s32[]{:S(2)}) async-start(s8[8388608]{0:T(1024)(128)(4,1)} %bitcast.113), calls=%async_computation.4 | async-start | bytes 8388608
  495.6 11.8 %slice-start.1 = ((s8[8388608]{0:T(1024)(128)(4,1)}), s8[4194304]{0:T(1024)(128)(4,1)S(1)}, s32[]{:S(2)}) async-start(s8[8388608]{0:T(1024)(128)(4,1)} %bitcast.113), calls=%async_computation.5 | async-start | bytes 8388608
  518.4 17.5 %copy-start.3 = (f32[2,1200,64]{1,2,0:T(8,128)S(1)}, f32[2,1200,64]{1,2,0:T(8,128)}, u32[]{:S(2)}) copy-start(f32[2,1200,64]{1,2,0:T(8,128)} %param.12) | copy-start | bytes 1843204
  518.4 17.5 %copy-start.4 = (f32[1200]{0:T(1024)S(1)}, f32[1200]{0:T(1024)}, u32[]{:S(2)}) copy-start(f32[1200]{0:T(1024)} %param.10) | copy-start | bytes 14404
Sparse Core Ops, SparseCore 0:
  416.0 85.2 all-gather.6
  582.5 85.6 all-gather.8
